TPU v7x, 32 devices: a whole 2x2x4 slice. The times are simulated.
32 devices in a mesh: gx: 4 (over z), gy: 8 (over y, x, core).
Axes of the slice: x: 2, y: 2, z: 4, core: 2. Of those that a mesh axis runs over, the one named last changes fastest.
Arguments:
- field: float32 [256, 3072], P('gx', 'gy'), may hold values from -9 to 9
- decay_x: float32 [256, 8], P('gx'), may hold values from 0.15 to 0.99999
- decay_y: float32 [384, 8], P('gy'), may hold values from 0.15 to 0.99999
Outputs:
- smoothed: float32 [256, 3072], P('gx', 'gy')
All inputs are finite; a program needn't handle non-finite values.
Results may differ from a plain program's by a relative error of at most 0.0003.
Values sent between devices are 32-bit elements; how exact they have to be, the bound alone decides.
A program may use at most 64 MiB of HBM per device.

v0:
```python
import jax
import jax.numpy as jnp
from jax import lax
from jax.sharding import PartitionSpec as P


def prefix_2(shard, axis, combine, identity, reverse):
    devices, mine = (lax.axis_size(axis), lax.axis_index(axis))
    everything = jax.tree.map(lambda part: lax.all_gather(part, axis), shard)
    start = jax.tree.map(
        lambda part, zero: jnp.broadcast_to(jnp.asarray(zero, part.dtype), part.shape),
        shard,
        identity,
    )

    def lap(k, before):
        at = devices - 1 - k if reverse else k
        reached = at > mine if reverse else at < mine
        new = combine(before, jax.tree.map(lambda part: part[at], everything))
        return jax.tree.map(lambda a, b: jnp.where(reached, a, b), new, before)

    return lax.fori_loop(0, devices, lap, start)


def local_operator(decay_factors, backward):
    if backward:
        decay_factors = decay_factors[::-1]
    count = decay_factors.shape[0]
    logs = jnp.log(decay_factors).T
    running = jnp.cumsum(logs, axis=1)
    grid_location = jnp.arange(count)
    lower = (grid_location[:, None] >= grid_location[None, :])[None]
    spread = running[:, :, None] - running[:, None, :]
    matrix = (
        jnp.where(lower, jnp.exp(jnp.where(lower, spread, 0.0)), 0.0)
        * (1.0 - decay_factors).T[:, None, :]
    )
    carried = jnp.exp(running)
    responses = [carried]
    for order in range(3):
        responses.append(
            jnp.einsum("lij,lj->li", matrix, responses[-1], precision=lax.Precision.HIGHEST)
        )
    response = jnp.stack(responses)
    if backward:
        matrix = matrix[:, ::-1, ::-1]
        response = response[:, :, ::-1]
    return (matrix, response)


def section_outputs(values, matrix, axis):
    form = "lij,jwl->iwl" if axis == 0 else "lij,wjl->wil"
    outputs = []
    current = values
    for order in range(4):
        current = jnp.einsum(form, matrix, current, precision=lax.Precision.HIGHEST)
        outputs.append(current)
    return outputs


def end_map(response, edge):
    edges = response[:, :, edge]
    empty = jnp.zeros_like(edges[0])
    rows = [
        jnp.stack(
            [edges[outer - inner] if inner <= outer else empty for inner in range(4)], axis=-1
        )
        for outer in range(4)
    ]
    return jnp.stack(rows, axis=1)


def compose(earlier, later):
    first_map, first_values = earlier
    second_map, second_values = later
    joined = jnp.einsum("lkm,lmn->lkn", second_map, first_map, precision=lax.Precision.HIGHEST)
    moved = (
        jnp.einsum("lkm,mwl->kwl", second_map, first_values, precision=lax.Precision.HIGHEST)
        + second_values
    )
    return (joined, moved)


def correction(response, state, axis):
    form = "mli,mwl->iwl" if axis == 0 else "mli,mwl->wil"
    return jnp.einsum(form, response[::-1], state, precision=lax.Precision.HIGHEST)


def carry_sweep(values, operator, axis, backward):
    matrix, response = operator
    edge = 0 if backward else matrix.shape[1] - 1
    outputs = section_outputs(values, matrix, axis)
    ends = jnp.stack([lax.index_in_dim(section, edge, axis, keepdims=False) for section in outputs])
    mapping = end_map(response, edge)
    start = (jnp.broadcast_to(jnp.eye(4, dtype=jnp.float32), mapping.shape), jnp.zeros_like(ends))
    if axis == 0:
        prefix = prefix_2((mapping, ends), "gx", compose, start, backward)
    else:
        prefix = prefix_2((mapping, ends), "gy", compose, start, backward)
    return outputs[3] + correction(response, prefix[1], axis)


def body(field, decay_x, decay_y):
    rows_x = decay_x.shape[0]
    levels = decay_x.shape[1]
    rows_y = decay_y.shape[0]
    grid = field.reshape(rows_x, rows_y, levels)
    forward_x = local_operator(decay_x, False)
    backward_x = local_operator(decay_x, True)
    forward_y = local_operator(decay_y, False)
    backward_y = local_operator(decay_y, True)
    grid = carry_sweep(grid, forward_x, 0, False)
    grid = carry_sweep(grid, backward_x, 0, True)
    grid = carry_sweep(grid, forward_y, 1, False)
    grid = carry_sweep(grid, backward_y, 1, True)
    return grid.reshape(rows_x, rows_y * levels)


def solution(mesh):
    placed = (P("gx", "gy"), P("gx", None), P("gy", None))
    return jax.shard_map(body, mesh=mesh, in_specs=placed, out_specs=P("gx", "gy"), check_vma=False)
```

profile of v0, /device:TPU:0, one launch (start us, length us, event | category | flops | bytes accessed | tf_op | source)
XLA Modules:
  0.0 127.3 jit_solution(12243400850540259673)
XLA Ops:
  0.1 0.6 copy-done.1
  0.8 0.6 copy-done.2
  1.5 0.2 reduce_window_sum.37
  1.7 0.2 reduce_window_sum.35
  1.9 0.6 fusion.46
  2.6 0.2 slice_reduce_fusion.10
  2.9 0.6 fusion.45
  3.6 0.2 slice_reduce_fusion.9
  3.8 0.6 fusion.44
  4.4 0.2 slice_reduce_fusion.8
  4.7 0.5 fusion.99
  5.2 0.2 slice_reduce_fusion.2
  5.6 0.5 fusion.98
  6.1 0.2 slice_reduce_fusion.1
  6.3 0.5 fusion.97
  6.8 0.2 slice_reduce_fusion
  7.1 0.2 reduce_window_sum.34
  7.4 0.6 fusion.28
  8.4 0.6 fusion.27
  9.0 0.2 slice_reduce_fusion.13
  9.2 0.6 fusion.26
  10.3 0.2 reduce_window_sum.36
  10.5 0.5 fusion.42
  11.0 0.2 slice_reduce_fusion.6
  11.4 0.5 fusion.41
  11.9 0.2 slice_reduce_fusion.5
  12.1 0.5 fusion.40
  12.6 0.2 slice_reduce_fusion.4
  13.3 14.9 %all-gather.2 = f32[32,4,4]{2,1,0:T(4,128)S(1)} all-gather(f32[8,4,4]{2,1,0:T(4,128)S(1)} %copy.75), channel_id=4, replica_groups=mesh['gx'=4,'gy'=8] {'gx'}, dimensions={0}, use_global_device_ids=true | all-gather | bytes 2560 | tf_op jit(solution)/shard_map/all_gather | solution.py:9
  28.4 13.3 %all-gather = f32[32,4,4]{2,1,0:T(4,128)S(1)} all-gather(f32[8,4,4]{2,1,0:T(4,128)S(1)} %copy.67), channel_id=2, replica_groups=mesh['gx'=4,'gy'=8] {'gx'}, dimensions={0}, use_global_device_ids=true | all-gather | bytes 2560 | tf_op jit(solution)/shard_map/all_gather | solution.py:9
  41.9 9.2 %all-gather.6 = f32[64,4,4]{2,1,0:T(4,128)S(1)} all-gather(f32[8,4,4]{2,1,0:T(4,128)S(1)} %copy.99), channel_id=8, replica_groups=mesh['gx'=4,'gy'=8] {'gy'}, dimensions={0}, use_global_device_ids=true | all-gather | bytes 4608 | tf_op jit(solution)/shard_map/all_gather | solution.py:9
  51.1 0.3 copy.100
  51.4 9.2 %all-gather.4 = f32[64,4,4]{2,1,0:T(4,128)S(1)} all-gather(f32[8,4,4]{2,1,0:T(4,128)S(1)} %copy.88), channel_id=6, replica_groups=mesh['gx'=4,'gy'=8] {'gy'}, dimensions={0}, use_global_device_ids=true | all-gather | bytes 4608 | tf_op jit(solution)/shard_map/all_gather | solution.py:9
  60.6 0.3 copy.89
  61.1 0.8 copy-done
  62.0 0.7 convolution_bitcast_fusion.13
  62.7 0.6 convolution_bitcast_fusion.12
  63.6 0.7 convolution_bitcast_fusion.11
  64.4 0.7 convolution_bitcast_fusion.10
  65.6 13.3 %all-gather.1 = f32[16,48,8]{1,2,0:T(8,128)S(1)} all-gather(f32[4,48,8]{1,2,0:T(8,128)S(1)} %pad_maximum_fusion), channel_id=3, replica_groups=mesh['gx'=4,'gy'=8] {'gx'}, dimensions={0}, use_global_device_ids=true | all-gather | bytes 30720 | tf_op jit(solution)/shard_map/all_gather | solution.py:9
  78.9 1.4 %while.60 = (s32[]{:T(128)}, f32[4,48,8]{1,0,2:T(4,128)S(1)}, s32[]{:T(128)}, f32[4,8,4,4]{1,3,2,0:T(4,128)S(1)}, f32[4,4,48,8]{2,3,1,0:T(8,128)S(1)}, /*index=5*/s32[]{:T(128)}, s32[]{:T(128)}) while((s32[]{:T(128)}, f32[4,48,8]{1,0,2:T(4,128)S(1)}, s32[]{:T(128)}, f32[4,8,4,4]{1,3,2,0:T(4,128)S(1)}, ...), condition=%wide.region_2.3_spmd.clone, body=%wide.region_1.2_spmd.clone.sunk | while | flops 79876 | bytes 45681 | solution.py:22
  80.3 0.5 fusion.25
  81.1 0.5 convolution_bitcast_fusion.9
  81.7 0.5 convolution_bitcast_fusion.8
  82.4 0.5 convolution_bitcast_fusion.7
  82.9 0.5 convolution_bitcast_fusion.6
  83.7 13.2 %all-gather.3 = f32[16,48,8]{1,2,0:T(8,128)S(1)} all-gather(f32[4,48,8]{1,2,0:T(8,128)S(1)} %pad_maximum_fusion.2), channel_id=5, replica_groups=mesh['gx'=4,'gy'=8] {'gx'}, dimensions={0}, use_global_device_ids=true | all-gather | bytes 30720 | tf_op jit(solution)/shard_map/all_gather | solution.py:9
  96.9 1.4 %while.61 = (s32[]{:T(128)}, f32[4,48,8]{1,0,2:T(4,128)S(1)}, s32[]{:T(128)}, f32[4,8,4,4]{1,3,2,0:T(4,128)S(1)}, f32[4,4,48,8]{2,3,1,0:T(8,128)S(1)}, /*index=5*/s32[]{:T(128)}, s32[]{:T(128)}, s32[]{:T(128)}, s32[]{:T(128)}) while((s32[]{:T(128)}, f32[4,48,8]{1,0,2:T(4,128)S(1)}, s32[]{:T(128)}, f32[4,8,4,4]{1,3,2,0:T(4,128)S(1)}, ...), condition=%wide.region_5.6_spmd.clone, body=%wide.region_4.5_spmd.clone.sunk | while | flops 79880 | bytes 45743 | solution.py:22
  98.3 0.5 fusion.24
  98.8 0.4 convolution_bitcast_fusion.5
  99.2 0.4 fusion.43
  99.6 0.4 fusion.36
  100.1 0.4 fusion.34
  100.6 8.2 %all-gather.5 = f32[32,64,8]{1,2,0:T(8,128)S(1)} all-gather(f32[4,64,8]{1,2,0:T(8,128)S(1)} %pad_maximum_fusion.4), channel_id=7, replica_groups=mesh['gx'=4,'gy'=8] {'gy'}, dimensions={0}, use_global_device_ids=true | all-gather | bytes 73728 | tf_op jit(solution)/shard_map/all_gather | solution.py:9
  108.9 2.8 %while.62 = (s32[]{:T(128)}, f32[4,64,8]{1,0,2:T(4,128)S(1)}, s32[]{:T(128)}, f32[8,8,4,4]{1,3,2,0:T(4,128)S(1)}, f32[8,4,64,8]{2,3,1,0:T(8,128)S(1)}, /*index=5*/s32[]{:T(128)}, s32[]{:T(128)}) while((s32[]{:T(128)}, f32[4,64,8]{1,0,2:T(4,128)S(1)}, s32[]{:T(128)}, f32[8,8,4,4]{1,3,2,0:T(4,128)S(1)}, ...), condition=%wide.region_8.9_spmd.clone, body=%wide.region_7.8_spmd.clone.sunk | while | flops 106500 | bytes 60017 | solution.py:22
  111.7 0.5 fusion.152
  112.3 0.3 convolution_bitcast_fusion.4
  112.6 0.3 fusion.200
  113.0 0.3 fusion.32
  113.3 0.3 fusion.30
  113.9 9.2 %all-gather.7 = f32[32,64,8]{1,2,0:T(8,128)S(1)} all-gather(f32[4,64,8]{1,2,0:T(8,128)S(1)} %pad_maximum_fusion.6), channel_id=9, replica_groups=mesh['gx'=4,'gy'=8] {'gy'}, dimensions={0}, use_global_device_ids=true | all-gather | bytes 73728 | tf_op jit(solution)/shard_map/all_gather | solution.py:9
  123.1 2.8 %while.63 = (s32[]{:T(128)}, f32[4,64,8]{1,0,2:T(4,128)S(1)}, s32[]{:T(128)}, f32[8,8,4,4]{1,3,2,0:T(4,128)S(1)}, f32[8,4,64,8]{2,3,1,0:T(8,128)S(1)}, /*index=5*/s32[]{:T(128)}, s32[]{:T(128)}, s32[]{:T(128)}, s32[]{:T(128)}) while((s32[]{:T(128)}, f32[4,64,8]{1,0,2:T(4,128)S(1)}, s32[]{:T(128)}, ...), condition=%wide.region_11.12_spmd.clone, body=%wide.region_10.11_spmd.clone.sunk | while | flops 106504 | bytes 60079 | solution.py:22
  125.9 0.5 fusion.150
  126.5 0.8 copy.104
  (205 shorter events, 12.6 us)
Async XLA Ops:
  0.0 0.7 copy-start.1
  0.7 0.7 copy-start.2
  61.0 0.9 copy-start
where the time goes:
time: 128 us; the launch traced here: 127 us
  blocking collectives  90.6 us (71%)
  matrix products  21 us (16%)
  local copies, waits for them, and re-layouts  12.4 us (10%)
  other arithmetic  1.72 us (1%)
    all_gather x8, blocking collectives, prefix_2(): everything = jax.tree.map(lambda part: lax.all_gather(part, axis), shard)  90.6 us
    dot_general x16, matrix products, section_outputs(): current = jnp.einsum(form, matrix, current, precision=lax.Precision.HIGHEST)  7.46 us
    dot_general x12, matrix products, local_operator(): jnp.einsum('lij,lj->li', matrix, responses[-1], precision=lax.Precision.H...  6.96 us
    dot_general x24, matrix products, compose(): jnp.einsum('lkm,mwl->kwl', second_map, first_values, precision=lax.Precis...  4.5 us
    slice x16, local copies, waits for them, and re-layouts, end_map(): edges[outer - inner]  3.01 us
    unnamed x11, local copies, waits for them, and re-layouts  2.97 us
    squeeze x48, local copies, waits for them, and re-layouts, lap(): new = combine(before, jax.tree.map(lambda part: part[at], everything))  2.74 us

commit v1 on v0

v1 whole, which is shorter than its diff:
```python
import functools

import jax
import jax.numpy as jnp
from jax import lax
from jax.experimental import pallas as pl
from jax.experimental.pallas import tpu as pltpu
from jax.sharding import PartitionSpec as P

LANES = 128
SUB = 8
HIGHEST = lax.Precision.HIGHEST
UNROLL = 8


def iota(dimension):
    return lax.broadcasted_iota(jnp.int32, (SUB, LANES), dimension)


def rows_of(i):
    return pl.ds(pl.multiple_of(i * SUB, SUB), SUB)


def spread(row):
    return jnp.broadcast_to(row, (SUB, LANES))


def sweep(count, slots, decay, load, mid, emit):
    sub = iota(0)
    zero = jnp.zeros((SUB, LANES), jnp.float32)

    def advance(i, states, value):
        a = decay[pl.ds(i, 1), :]
        g = 1.0 - a
        result = []
        for state in states:
            value = a * state + g * value
            result.append(value)
        return tuple(result)

    def forward(i, states):
        states = advance(i, states, load(i))
        kept = states[3]
        for order in range(3):
            kept = jnp.where(sub == slots + 1 + order, states[order], kept)
        mid[rows_of(i), :] = kept
        return states

    def backward(i, states):
        states = advance(i, states, mid[rows_of(i), :])
        emit(i, states)
        return states

    def chunks(step, states, reverse):
        width = UNROLL if count % UNROLL == 0 else 1

        def chunk(j, states):
            for u in range(width):
                i = j * width + u
                states = step(count - 1 - i if reverse else i, states)
            return states

        return lax.fori_loop(0, count // width, chunk, states)

    one = jnp.where(sub > slots, 1.0, 0.0)
    first = chunks(forward, (one, zero, zero, zero), False)
    one = jnp.where(sub == slots, 1.0, 0.0)
    second = chunks(backward, (one, zero, zero, zero), True)
    return first, second


def compose(devices, mine, slots, ends, maps):
    zero = jnp.zeros((SUB, LANES), jnp.float32)
    state = [zero] * 4
    entering = []
    picked = [zero] * 4
    for p in range(devices):
        entering.append(state)
        picked = [jnp.where(mine == p, new, old) for new, old in zip(state, picked)]
        if p == devices - 1:
            break
        r = [maps(p, k)[slots + 1 : slots + 2, :] for k in range(4)]
        state = [
            ends(p, k) + sum(r[k - m] * state[m] for m in range(k + 1)) for k in range(4)
        ]
    ahead = picked
    state = [zero] * 4
    picked = [zero] * 4
    for p in range(devices - 1, -1, -1):
        picked = [jnp.where(mine == p, new, old) for new, old in zip(state, picked)]
        if p == 0:
            break
        back = [maps(p, 4 + k) for k in range(4)]
        r = [back[k][slots : slots + 1, :] for k in range(4)]
        before = entering[p]
        state = [
            ends(p, 4 + k)
            + sum(r[k - m] * state[m] for m in range(k + 1))
            + sum(back[k][slots + 4 - m : slots + 5 - m, :] * before[m] for m in range(4))
            for k in range(4)
        ]
    return ahead, picked


def kernel(
    nx, ny, cx, cy, slots,
    field, decay_x, decay_y, out,
    ax, ay, xin, mid, xout, xresp, grid, wt, yacc,
    xsend, xrecv, msend, mrecv, ysend, yrecv,
    xs, xr, ms, mr, ys, yr,
):
    levels = decay_x.shape[1]
    group = LANES // levels
    blocks = cx // SUB
    mx, my = lax.axis_index("gx"), lax.axis_index("gy")
    barrier = pltpu.get_barrier_semaphore()
    for d in range(1, nx):
        pl.semaphore_signal(barrier, inc=1, device_id=(lax.rem(mx + d, nx), my), device_id_type=pl.DeviceIdType.MESH)
    for d in range(1, ny):
        pl.semaphore_signal(barrier, inc=1, device_id=(mx, lax.rem(my + d, ny)), device_id_type=pl.DeviceIdType.MESH)

    sub, lane = iota(0), iota(1)
    lane_group = lane // levels
    tiling = jnp.where(
        lax.broadcasted_iota(jnp.int32, (levels, LANES), 1) % levels
        == lax.broadcasted_iota(jnp.int32, (levels, LANES), 0),
        1.0,
        0.0,
    )
    ax[...] = jnp.dot(decay_x[...], tiling, precision=HIGHEST, preferred_element_type=jnp.float32)
    ay[...] = jnp.dot(decay_y[...], tiling, precision=HIGHEST, preferred_element_type=jnp.float32)
    for b in range(blocks):
        for s in range(slots):
            xin[pl.ds(b * SUB * SUB + s, SUB, stride=SUB), :] = field[
                b * SUB : (b + 1) * SUB, s * LANES : (s + 1) * LANES
            ]

    def emit_x(i, states):
        xout[rows_of(i), :] = states[3]
        for order in range(3):
            xresp[order, rows_of(i), :] = states[order]

    first, second = sweep(
        cx, slots, ax, lambda i: jnp.where(sub < slots, xin[rows_of(i), :], 0.0), mid, emit_x
    )
    for k in range(4):
        xsend[k] = first[k]
        xsend[4 + k] = second[k]
        xrecv[mx, k] = first[k]
        xrecv[mx, 4 + k] = second[k]

    pl.semaphore_wait(barrier, nx + ny - 2)

    def along_x(d):
        return (lax.rem(mx + d, nx), my), lax.rem(mx + d, nx)

    def along_y(d):
        return (mx, lax.rem(my + d, ny)), lax.rem(my + d, ny)

    def copies(count, mine, along, src, dst, ssem, rsem):
        sends, receives = [], []
        for d in range(1, count):
            where, index = along(d)
            sends.append(
                pltpu.make_async_remote_copy(
                    src_ref=src, dst_ref=dst.at[mine], send_sem=ssem.at[d], recv_sem=rsem.at[mine],
                    device_id=where, device_id_type=pl.DeviceIdType.MESH,
                )
            )
            receives.append(
                pltpu.make_async_remote_copy(
                    src_ref=src, dst_ref=dst.at[index], send_sem=ssem.at[d], recv_sem=rsem.at[index],
                    device_id=where, device_id_type=pl.DeviceIdType.MESH,
                )
            )
        return sends, receives

    x_sends, x_receives = copies(nx, mx, along_x, xsend, xrecv, xs, xr)
    m_sends, m_receives = copies(ny, my, along_y, msend, mrecv, ms, mr)
    y_sends, y_receives = copies(ny, my, along_y, ysend, yrecv, ys, yr)
    for copy in x_sends:
        copy.start()

    own_level = lane % levels == sub
    yacc[...] = jnp.zeros_like(yacc)

    def impulse(i):
        return jnp.where(
            (sub < slots) & (sub * LANES + lane >= i * levels) & (sub * LANES + lane < (i + 1) * levels),
            1.0,
            0.0,
        )

    def emit_y(i, states):
        for s in range(slots):
            wt[rows_of(i), s * LANES : (s + 1) * LANES] = jnp.where(
                own_level, spread(states[3][s : s + 1, :]), 0.0
            )
        here = lane_group == lax.rem(i, group)
        chunk = i // group
        for order in range(4):
            yacc[order, chunk] = jnp.where(here, states[order], yacc[order, chunk])

    first, second = sweep(cy, slots, ay, impulse, mid, emit_y)
    for k in range(4):
        msend[k] = first[k]
        msend[4 + k] = second[k]
        mrecv[my, k] = first[k]
        mrecv[my, 4 + k] = second[k]
    for copy in m_sends:
        copy.start()
    y_ends = first + second

    for copy in x_receives:
        copy.wait_recv()
    ahead, behind = compose(nx, mx, slots, lambda p, k: xrecv[p, k], lambda p, k: xrecv[p, k])

    def tile(ref, b, s):
        return ref[pl.ds(b * SUB * SUB + s, SUB, stride=SUB), :]

    sums = []
    for b in range(blocks):
        parts = []
        g = [tile(xout, b, slots + 4 - m) for m in range(4)]
        r = [tile(xout, b, slots)] + [tile(xresp.at[2 - m], b, slots) for m in range(3)]
        for s in range(slots):
            value = tile(xout, b, s)
            for m in range(4):
                value = value + g[m] * ahead[m][s : s + 1, :] + r[m] * behind[m][s : s + 1, :]
            grid[b * SUB : (b + 1) * SUB, s * LANES : (s + 1) * LANES] = value
            parts.append(value)
        sums.append(parts)

    merge = jnp.where(
        lax.broadcasted_iota(jnp.int32, (LANES, LANES), 0) % levels
        == lax.broadcasted_iota(jnp.int32, (LANES, LANES), 1) % levels,
        1.0,
        0.0,
    )
    products = [
        sum(sums[b][s] * y_ends[k][s : s + 1, :] for s in range(slots))
        for k in range(8)
        for b in range(blocks)
    ]
    totals = jnp.dot(
        jnp.concatenate(products, axis=0), merge, precision=HIGHEST, preferred_element_type=jnp.float32
    )
    for k in range(8):
        packed = jnp.zeros((SUB, LANES), jnp.float32)
        for b in range(blocks):
            at = (k * blocks + b) * SUB
            packed = jnp.where(lane_group == b, totals[at : at + SUB, :], packed)
        ysend[k] = packed
        yrecv[my, k] = packed
    for copy in y_sends:
        copy.start()

    out[...] = lax.dot_general(
        grid[...], wt[...], (((1,), (1,)), ((), ())), precision=HIGHEST, preferred_element_type=jnp.float32
    )

    for copy in m_receives:
        copy.wait_recv()
    for copy in y_receives:
        copy.wait_recv()
    ahead, behind = compose(ny, my, slots, lambda p, k: yrecv[p, k], lambda p, k: mrecv[p, k])
    states = list(ahead) + list(behind)
    masked = [jnp.where(lane_group == b, states[m], 0.0) for m in range(8) for b in range(blocks)]
    opened = jnp.dot(
        jnp.concatenate(masked, axis=0), merge, precision=HIGHEST, preferred_element_type=jnp.float32
    )
    for s in range(slots):
        held = [yacc[order, s] for order in range(4)]
        answers = [held[3][slots + 4 - m : slots + 5 - m, :] for m in range(4)]
        answers += [held[3 - m][slots : slots + 1, :] for m in range(4)]
        for b in range(blocks):
            value = out[b * SUB : (b + 1) * SUB, s * LANES : (s + 1) * LANES]
            for m in range(8):
                at = (m * blocks + b) * SUB
                value = value + opened[at : at + SUB, :] * answers[m]
            out[b * SUB : (b + 1) * SUB, s * LANES : (s + 1) * LANES] = value
    for copy in x_sends + m_sends + y_sends:
        copy.wait_send()


def body(nx, ny, field, decay_x, decay_y):
    cx, levels = decay_x.shape
    cy = decay_y.shape[0]
    width = cy * levels
    slots = -(-width // LANES)
    padded = slots * LANES
    if padded != width:
        field = jnp.pad(field, ((0, 0), (0, padded - width)))
    longest = max(cx, cy)
    vmem = lambda *shape: pltpu.VMEM(shape, jnp.float32)
    dma = pltpu.SemaphoreType.DMA
    result = pl.pallas_call(
        functools.partial(kernel, nx, ny, cx, cy, slots),
        out_shape=jax.ShapeDtypeStruct((cx, padded), jnp.float32),
        in_specs=[pl.BlockSpec(memory_space=pltpu.VMEM)] * 3,
        out_specs=pl.BlockSpec(memory_space=pltpu.VMEM),
        scratch_shapes=[
            vmem(cx, LANES),
            vmem(cy, LANES),
            vmem(cx * SUB, LANES),
            vmem(longest * SUB, LANES),
            vmem(cx * SUB, LANES),
            vmem(3, cx * SUB, LANES),
            vmem(cx, padded),
            vmem(padded, padded),
            vmem(4, slots, SUB, LANES),
            vmem(8, SUB, LANES),
            vmem(nx, 8, SUB, LANES),
            vmem(8, SUB, LANES),
            vmem(ny, 8, SUB, LANES),
            vmem(8, SUB, LANES),
            vmem(ny, 8, SUB, LANES),
            dma((nx,)),
            dma((nx,)),
            dma((ny,)),
            dma((ny,)),
            dma((ny,)),
            dma((ny,)),
        ],
        compiler_params=pltpu.CompilerParams(collective_id=0, has_side_effects=True),
    )(field, decay_x, decay_y)
    return result[:, :width] if padded != width else result


def solution(mesh):
    placed = (P("gx", "gy"), P("gx", None), P("gy", None))
    nx, ny = mesh.shape["gx"], mesh.shape["gy"]
    return jax.shard_map(
        functools.partial(body, nx, ny), mesh=mesh, in_specs=placed, out_specs=P("gx", "gy"), check_vma=False
    )
```

time: 128 us -> 19.8 us (0.15)
  blocking collectives: 90.6 us -> 0 us
  matrix products: 21 us -> 0 us
  Pallas kernels: 0 us -> 15.9 us
  local copies, waits for them, and re-layouts: 12.4 us -> 3.63 us
  other arithmetic: 1.72 us -> 0 us
    all_gather x8 -> x0, blocking collectives: 90.6 us -> none  [prefix_2(): everything = jax.tree.map(lambda part: lax.all_gather(part, axis), shard)]
    dot_general x56 -> x0, matrix products: 21 us -> none  [the longest x16 7.46 us: section_outputs(): current = jnp.einsum(form, matrix, current, precision=lax.Precision.HIGHEST)]
    pallas_call x0 -> x1, Pallas kernels: none -> 15.9 us  [body(): pl.pallas_call(functools.partial(kernel, nx, ny, cx, cy, slots), out_shap...]
    slice x30 -> x0, local copies, waits for them, and re-layouts: 4.29 us -> none  [the longest x16 3.01 us: end_map(): edges[outer - inner]]
    squeeze x48 -> x0, local copies, waits for them, and re-layouts: 2.74 us -> none  [lap(): new = combine(before, jax.tree.map(lambda part: part[at], everything))]
    unnamed x11 -> x5, local copies, waits for them, and re-layouts: 2.97 us -> 3.63 us
where the time goes in v1:
time: 19.8 us; the launch traced here: 19.6 us
  Pallas kernels  15.9 us (80%)
  local copies, waits for them, and re-layouts  3.63 us (18%)
    pallas_call x1, Pallas kernels, body(): pl.pallas_call(functools.partial(kernel, nx, ny, cx, cy, slots), out_shap...  15.9 us
    unnamed x5, local copies, waits for them, and re-layouts  3.63 us

profile of v1, /device:TPU:0, one launch (start us, length us, event | category | flops | bytes accessed | tf_op | source)
XLA Modules:
  0.0 19.6 jit_solution(3141743590536212395)
XLA Ops:
  0.0 0.0 copy-start
  0.0 1.4 %copy.5.decay_y = f32[48,8]{1,0:T(8,128)} copy(f32[48,8]{0,1:T(8,128)} %param.5) | data formatting | bytes 3072 | tf_op args[2]
  1.4 0.0 copy-done
  1.4 0.7 %copy.4.decay_x = f32[64,8]{1,0:T(8,128)} copy(f32[64,8]{0,1:T(8,128)S(1)} %copy-done) | data formatting | bytes 4096 | tf_op args[1]
  2.1 15.9 %shard_map.37 = f32[64,384]{1,0:T(8,128)} custom-call(f32[64,384]{1,0:T(8,128)} %field.1, f32[64,8]{1,0:T(8,128)} %copy.4.decay_x, f32[48,8]{1,0:T(8,128)} %copy.5.decay_y), custom_call_target="tpu_custom_call" | custom-call | tf_op jit(solution)/shard_map/pallas_call | solution.py:297
  18.0 1.5 %copy.7 = f32[64,384]{1,0:T(8,128)} copy(f32[64,384]{1,0:T(8,128)} %shard_map.37) | data formatting | bytes 196608
Async XLA Ops:
  0.0 1.4 %copy-start = (f32[64,8]{0,1:T(8,128)S(1)}, f32[64,8]{0,1:T(8,128)}, u32[]{:S(2)}) copy-start(f32[64,8]{0,1:T(8,128)} %param.4) | copy-start | bytes 6148

commit v2 on v1

--- a/solution.py
+++ b/solution.py
@@ -10,7 +10,7 @@
 LANES = 128
 SUB = 8
 HIGHEST = lax.Precision.HIGHEST
-UNROLL = 8
+UNROLL = 16
 
 
 def iota(dimension):
@@ -67,6 +67,50 @@
     one = jnp.where(sub == slots, 1.0, 0.0)
     second = chunks(backward, (one, zero, zero, zero), True)
     return first, second
+
+
+def pack_maps(first, second, lane_group):
+    packed = second[0]
+    for k in range(1, 8):
+        packed = jnp.where(lane_group == k, (second + first)[k], packed)
+    return packed
+
+
+def open_map(packed, k, lane_group, levels):
+    value = jnp.where(lane_group == (k + 4) % 8, packed, 0.0)
+    shift = levels
+    while shift < LANES:
+        value = value + pltpu.roll(value, shift, 1)
+        shift *= 2
+    return value
+
+
+def pack_ends(ends, packed, slots):
+    sub = iota(0)
+    half = SUB // 2
+    result = [
+        jnp.where(sub < half, ends[2 * v], pltpu.roll(ends[2 * v + 1], half, 0)) for v in range(4)
+    ]
+    for v, at, row in map_rows(slots):
+        result[v] = jnp.where(sub == at, packed[row : row + 1, :], result[v])
+    return result
+
+
+def map_rows(slots):
+    half = SUB // 2
+    last = half - 1
+    return (
+        (0, last, slots + 1),
+        (1, last, slots),
+        (2, last, slots + 2),
+        (2, half + last, slots + 3),
+        (3, last, slots + 4),
+    )
+
+
+def open_ends(vectors, k):
+    vector = vectors[k // 2]
+    return pltpu.roll(vector, SUB // 2, 0) if k % 2 else vector
 
 
 def compose(devices, mine, slots, ends, maps):
@@ -104,12 +148,12 @@
 
 def kernel(
     nx, ny, cx, cy, slots,
-    field, decay_x, decay_y, out,
-    ax, ay, xin, mid, xout, xresp, grid, wt, yacc,
+    field, decay_x_in, decay_y_in, out,
+    decay_x, decay_y, ax, ay, xin, mid, xout, xresp, grid, wt, yacc,
     xsend, xrecv, msend, mrecv, ysend, yrecv,
-    xs, xr, ms, mr, ys, yr,
+    xs, xr, ms, mr, ys, yr, xs_back, xr_back, ys_back, yr_back, loaded,
 ):
-    levels = decay_x.shape[1]
+    levels = decay_x.shape[0]
     group = LANES // levels
     blocks = cx // SUB
     mx, my = lax.axis_index("gx"), lax.axis_index("gy")
@@ -119,6 +163,17 @@
     for d in range(1, ny):
         pl.semaphore_signal(barrier, inc=1, device_id=(mx, lax.rem(my + d, ny)), device_id_type=pl.DeviceIdType.MESH)
 
+    loads = [
+        pltpu.make_async_copy(decay_x_in, decay_x, loaded.at[0]),
+        pltpu.make_async_copy(decay_y_in, decay_y, loaded.at[1]),
+    ]
+    loads += [
+        pltpu.make_async_copy(field.at[:, pl.ds(s * LANES, LANES)], xin.at[:, s], loaded.at[2 + s])
+        for s in range(slots)
+    ]
+    for copy in loads:
+        copy.start()
+
     sub, lane = iota(0), iota(1)
     lane_group = lane // levels
     tiling = jnp.where(
@@ -127,13 +182,13 @@
         1.0,
         0.0,
     )
-    ax[...] = jnp.dot(decay_x[...], tiling, precision=HIGHEST, preferred_element_type=jnp.float32)
-    ay[...] = jnp.dot(decay_y[...], tiling, precision=HIGHEST, preferred_element_type=jnp.float32)
-    for b in range(blocks):
-        for s in range(slots):
-            xin[pl.ds(b * SUB * SUB + s, SUB, stride=SUB), :] = field[
-                b * SUB : (b + 1) * SUB, s * LANES : (s + 1) * LANES
-            ]
+    for copy, target, source in ((loads[0], ax, decay_x), (loads[1], ay, decay_y)):
+        copy.wait()
+        target[...] = lax.dot_general(
+            source[...], tiling, (((0,), (0,)), ((), ())), precision=HIGHEST, preferred_element_type=jnp.float32
+        )
+    for copy in loads[2:]:
+        copy.wait()
 
     def emit_x(i, states):
         xout[rows_of(i), :] = states[3]
@@ -141,13 +196,12 @@
             xresp[order, rows_of(i), :] = states[order]
 
     first, second = sweep(
-        cx, slots, ax, lambda i: jnp.where(sub < slots, xin[rows_of(i), :], 0.0), mid, emit_x
+        cx, slots, ax, lambda i: jnp.where(sub < slots, xin[i], 0.0), mid, emit_x
     )
-    for k in range(4):
-        xsend[k] = first[k]
-        xsend[4 + k] = second[k]
-        xrecv[mx, k] = first[k]
-        xrecv[mx, 4 + k] = second[k]
+    packed = pack_maps(first, second, lane_group)
+    for v, vector in enumerate(pack_ends(first + second, packed, slots)):
+        xsend[v] = vector
+        xrecv[mx, v] = vector
 
     pl.semaphore_wait(barrier, nx + ny - 2)
 
@@ -156,6 +210,31 @@
 
     def along_y(d):
         return (mx, lax.rem(my + d, ny)), lax.rem(my + d, ny)
+
+    def both_ways(count, mine, along, src, dst, ssem, rsem, ssem_back, rsem_back):
+        half = src.shape[0] // 2
+        ahead, back = pl.ds(0, half), pl.ds(half, half)
+        sends, receives = copies(count, mine, along, src.at[ahead], dst.at[:, ahead], ssem, rsem)
+        sends_back, receives_back = copies(
+            count, mine, along, src.at[back], dst.at[:, back], ssem_back, rsem_back
+        )
+
+        def start():
+            for d in range(1, count):
+                sends[d - 1].start()
+                pl.when(mine + d >= count)(sends_back[d - 1].start)
+
+        def wait_receives():
+            for d in range(1, count):
+                receives[d - 1].wait_recv()
+                pl.when(mine + d < count)(receives_back[d - 1].wait_recv)
+
+        def wait_sends():
+            for d in range(1, count):
+                sends[d - 1].wait_send()
+                pl.when(mine + d >= count)(sends_back[d - 1].wait_send)
+
+        return start, wait_receives, wait_sends
 
     def copies(count, mine, along, src, dst, ssem, rsem):
         sends, receives = [], []
@@ -175,11 +254,10 @@
             )
         return sends, receives
 
-    x_sends, x_receives = copies(nx, mx, along_x, xsend, xrecv, xs, xr)
+    x_start, x_wait, x_finish = both_ways(nx, mx, along_x, xsend, xrecv, xs, xr, xs_back, xr_back)
     m_sends, m_receives = copies(ny, my, along_y, msend, mrecv, ms, mr)
-    y_sends, y_receives = copies(ny, my, along_y, ysend, yrecv, ys, yr)
-    for copy in x_sends:
-        copy.start()
+    y_start, y_wait, y_finish = both_ways(ny, my, along_y, ysend, yrecv, ys, yr, ys_back, yr_back)
+    x_start()
 
     own_level = lane % levels == sub
     yacc[...] = jnp.zeros_like(yacc)
@@ -202,18 +280,23 @@
             yacc[order, chunk] = jnp.where(here, states[order], yacc[order, chunk])
 
     first, second = sweep(cy, slots, ay, impulse, mid, emit_y)
-    for k in range(4):
-        msend[k] = first[k]
-        msend[4 + k] = second[k]
-        mrecv[my, k] = first[k]
-        mrecv[my, 4 + k] = second[k]
+    packed = pack_maps(first, second, lane_group)
+    msend[...] = packed
+    mrecv[my] = packed
     for copy in m_sends:
         copy.start()
     y_ends = first + second
 
-    for copy in x_receives:
-        copy.wait_recv()
-    ahead, behind = compose(nx, mx, slots, lambda p, k: xrecv[p, k], lambda p, k: xrecv[p, k])
+    x_wait()
+    ends, maps = [], []
+    for p in range(nx):
+        vectors = [xrecv[p, v] for v in range(4)]
+        packed = vectors[0]
+        for v, at, row in map_rows(slots):
+            packed = jnp.where(sub == row, vectors[v][at : at + 1, :], packed)
+        ends.append([open_ends(vectors, k) for k in range(8)])
+        maps.append([open_map(packed, k, lane_group, levels) for k in range(8)])
+    ahead, behind = compose(nx, mx, slots, lambda p, k: ends[p][k], lambda p, k: maps[p][k])
 
     def tile(ref, b, s):
         return ref[pl.ds(b * SUB * SUB + s, SUB, stride=SUB), :]
@@ -236,24 +319,32 @@
         == lax.broadcasted_iota(jnp.int32, (LANES, LANES), 1) % levels,
         1.0,
         0.0,
-    )
+    ).astype(jnp.bfloat16)
+
+    def merged(parts):
+        rows = jnp.concatenate(parts, axis=0)
+        high = rows.astype(jnp.bfloat16)
+        low = (rows - high.astype(jnp.float32)).astype(jnp.bfloat16)
+        return jnp.dot(high, merge, preferred_element_type=jnp.float32) + jnp.dot(
+            low, merge, preferred_element_type=jnp.float32
+        )
+
     products = [
         sum(sums[b][s] * y_ends[k][s : s + 1, :] for s in range(slots))
         for k in range(8)
         for b in range(blocks)
     ]
-    totals = jnp.dot(
-        jnp.concatenate(products, axis=0), merge, precision=HIGHEST, preferred_element_type=jnp.float32
-    )
-    for k in range(8):
+    totals = merged(products)
+    shared = ysend.shape[0] < 8
+    for v in range(ysend.shape[0]):
         packed = jnp.zeros((SUB, LANES), jnp.float32)
-        for b in range(blocks):
-            at = (k * blocks + b) * SUB
-            packed = jnp.where(lane_group == b, totals[at : at + SUB, :], packed)
-        ysend[k] = packed
-        yrecv[my, k] = packed
-    for copy in y_sends:
-        copy.start()
+        for k, base in ((2 * v, 0), (2 * v + 1, group // 2)) if shared else ((v, 0),):
+            for b in range(blocks):
+                at = (k * blocks + b) * SUB
+                packed = jnp.where(lane_group == base + b, totals[at : at + SUB, :], packed)
+        ysend[v] = packed
+        yrecv[my, v] = packed
+    y_start()
 
     out[...] = lax.dot_general(
         grid[...], wt[...], (((1,), (1,)), ((), ())), precision=HIGHEST, preferred_element_type=jnp.float32
@@ -261,14 +352,19 @@
 
     for copy in m_receives:
         copy.wait_recv()
-    for copy in y_receives:
-        copy.wait_recv()
-    ahead, behind = compose(ny, my, slots, lambda p, k: yrecv[p, k], lambda p, k: mrecv[p, k])
+    maps = [[open_map(mrecv[p], k, lane_group, levels) for k in range(8)] for p in range(ny)]
+    y_wait()
+
+    def y_ends_of(p, k):
+        if not shared:
+            return yrecv[p, k]
+        vector = yrecv[p, k // 2]
+        return pltpu.roll(vector, LANES // 2, 1) if k % 2 else vector
+
+    ahead, behind = compose(ny, my, slots, y_ends_of, lambda p, k: maps[p][k])
     states = list(ahead) + list(behind)
     masked = [jnp.where(lane_group == b, states[m], 0.0) for m in range(8) for b in range(blocks)]
-    opened = jnp.dot(
-        jnp.concatenate(masked, axis=0), merge, precision=HIGHEST, preferred_element_type=jnp.float32
-    )
+    opened = merged(masked)
     for s in range(slots):
         held = [yacc[order, s] for order in range(4)]
         answers = [held[3][slots + 4 - m : slots + 5 - m, :] for m in range(4)]
@@ -279,7 +375,9 @@
                 at = (m * blocks + b) * SUB
                 value = value + opened[at : at + SUB, :] * answers[m]
             out[b * SUB : (b + 1) * SUB, s * LANES : (s + 1) * LANES] = value
-    for copy in x_sends + m_sends + y_sends:
+    x_finish()
+    y_finish()
+    for copy in m_sends:
         copy.wait_send()
 
 
@@ -292,38 +390,36 @@
     if padded != width:
         field = jnp.pad(field, ((0, 0), (0, padded - width)))
     longest = max(cx, cy)
+    halves = 4 if 2 * (cx // SUB) * levels <= LANES else 8
     vmem = lambda *shape: pltpu.VMEM(shape, jnp.float32)
     dma = pltpu.SemaphoreType.DMA
     result = pl.pallas_call(
         functools.partial(kernel, nx, ny, cx, cy, slots),
         out_shape=jax.ShapeDtypeStruct((cx, padded), jnp.float32),
-        in_specs=[pl.BlockSpec(memory_space=pltpu.VMEM)] * 3,
+        in_specs=[pl.BlockSpec(memory_space=pl.ANY)] * 3,
         out_specs=pl.BlockSpec(memory_space=pltpu.VMEM),
         scratch_shapes=[
+            vmem(levels, cx),
+            vmem(levels, cy),
             vmem(cx, LANES),
             vmem(cy, LANES),
-            vmem(cx * SUB, LANES),
+            vmem(cx, SUB, LANES),
             vmem(longest * SUB, LANES),
             vmem(cx * SUB, LANES),
             vmem(3, cx * SUB, LANES),
             vmem(cx, padded),
             vmem(padded, padded),
             vmem(4, slots, SUB, LANES),
-            vmem(8, SUB, LANES),
-            vmem(nx, 8, SUB, LANES),
-            vmem(8, SUB, LANES),
-            vmem(ny, 8, SUB, LANES),
-            vmem(8, SUB, LANES),
-            vmem(ny, 8, SUB, LANES),
-            dma((nx,)),
-            dma((nx,)),
-            dma((ny,)),
-            dma((ny,)),
-            dma((ny,)),
-            dma((ny,)),
+            vmem(4, SUB, LANES),
+            vmem(nx, 4, SUB, LANES),
+            vmem(SUB, LANES),
+            vmem(ny, SUB, LANES),
+            vmem(halves, SUB, LANES),
+            vmem(ny, halves, SUB, LANES),
+            *[dma((count,)) for count in (nx, nx, ny, ny, ny, ny, nx, nx, ny, ny, 2 + slots)],
         ],
         compiler_params=pltpu.CompilerParams(collective_id=0, has_side_effects=True),
-    )(field, decay_x, decay_y)
+    )(field, decay_x.T, decay_y.T)
     return result[:, :width] if padded != width else result
 
 

time: 19.8 us -> 16.5 us (0.83)
  local copies, waits for them, and re-layouts: 3.63 us -> 1.54 us
  Pallas kernels: 15.9 us -> 14.8 us
    unnamed x5 -> x1, local copies, waits for them, and re-layouts: 3.63 us -> 1.54 us
    pallas_call x1, Pallas kernels: 15.9 us -> 14.8 us  [body(): pl.pallas_call(functools.partial(kernel, nx, ny, cx, cy, slots), out_shap...]
where the time goes in v2:
time: 16.5 us; the launch traced here: 16.3 us
  Pallas kernels  14.8 us (90%)
  local copies, waits for them, and re-layouts  1.54 us (9%)
    pallas_call x1, Pallas kernels, body(): pl.pallas_call(functools.partial(kernel, nx, ny, cx, cy, slots), out_shap...  14.8 us
    unnamed x1, local copies, waits for them, and re-layouts  1.54 us

profile of v2, /device:TPU:0, one launch (start us, length us, event | category | flops | bytes accessed | tf_op | source)
XLA Modules:
  0.0 16.3 jit_solution(8535798605644289405)
XLA Ops:
  0.0 14.8 %shard_map.37 = f32[64,384]{1,0:T(8,128)} custom-call(f32[64,384]{1,0:T(8,128)} %field.1, f32[8,64]{1,0:T(8,128)} %bitcast.2, f32[8,48]{1,0:T(8,128)} %bitcast.3), custom_call_target="tpu_custom_call" | custom-call | tf_op jit(solution)/shard_map/pallas_call | solution.py:396
  14.8 1.5 %copy.5 = f32[64,384]{1,0:T(8,128)} copy(f32[64,384]{1,0:T(8,128)} %shard_map.37) | data formatting | bytes 196608

commit v3 on v2

--- a/solution.py
+++ b/solution.py
@@ -148,10 +148,10 @@
 
 def kernel(
     nx, ny, cx, cy, slots,
-    field, decay_x_in, decay_y_in, out,
-    decay_x, decay_y, ax, ay, xin, mid, xout, xresp, grid, wt, yacc,
+    field, decay_x_in, decay_y_in, result,
+    out,    decay_x, decay_y, ax, ay, xin, mid, xout, xresp, grid, wt, yacc,
     xsend, xrecv, msend, mrecv, ysend, yrecv,
-    xs, xr, ms, mr, ys, yr, xs_back, xr_back, ys_back, yr_back, loaded,
+    xs, xr, ms, mr, ys, yr, xs_back, xr_back, ys_back, yr_back, loaded, stored,
 ):
     levels = decay_x.shape[0]
     group = LANES // levels
@@ -365,6 +365,7 @@
     states = list(ahead) + list(behind)
     masked = [jnp.where(lane_group == b, states[m], 0.0) for m in range(8) for b in range(blocks)]
     opened = merged(masked)
+    stores = []
     for s in range(slots):
         held = [yacc[order, s] for order in range(4)]
         answers = [held[3][slots + 4 - m : slots + 5 - m, :] for m in range(4)]
@@ -375,10 +376,15 @@
                 at = (m * blocks + b) * SUB
                 value = value + opened[at : at + SUB, :] * answers[m]
             out[b * SUB : (b + 1) * SUB, s * LANES : (s + 1) * LANES] = value
+        columns = pl.ds(s * LANES, LANES)
+        stores.append(pltpu.make_async_copy(out.at[:, columns], result.at[:, columns], stored.at[s]))
+        stores[s].start()
     x_finish()
     y_finish()
     for copy in m_sends:
         copy.wait_send()
+    for copy in stores:
+        copy.wait()
 
 
 def body(nx, ny, field, decay_x, decay_y):
@@ -396,9 +402,10 @@
     result = pl.pallas_call(
         functools.partial(kernel, nx, ny, cx, cy, slots),
         out_shape=jax.ShapeDtypeStruct((cx, padded), jnp.float32),
-        in_specs=[pl.BlockSpec(memory_space=pl.ANY)] * 3,
-        out_specs=pl.BlockSpec(memory_space=pltpu.VMEM),
+        in_specs=[pl.BlockSpec(memory_space=pltpu.MemorySpace.HBM)] * 3,
+        out_specs=pl.BlockSpec(memory_space=pl.ANY),
         scratch_shapes=[
+            vmem(cx, padded),
             vmem(levels, cx),
             vmem(levels, cy),
             vmem(cx, LANES),
@@ -416,10 +423,10 @@
             vmem(ny, SUB, LANES),
             vmem(halves, SUB, LANES),
             vmem(ny, halves, SUB, LANES),
-            *[dma((count,)) for count in (nx, nx, ny, ny, ny, ny, nx, nx, ny, ny, 2 + slots)],
+            *[dma((count,)) for count in (nx, nx, ny, ny, ny, ny, nx, nx, ny, ny, 2 + slots, slots)],
         ],
-        compiler_params=pltpu.CompilerParams(collective_id=0, has_side_effects=True),
-    )(field, decay_x.T, decay_y.T)
+        compiler_params=pltpu.CompilerParams(collective_id=0, has_side_effects=True, vmem_limit_bytes=24 << 20),
+    )(*[pltpu.with_memory_space_constraint(v, pltpu.MemorySpace.HBM) for v in (field, decay_x.T, decay_y.T)])
     return result[:, :width] if padded != width else result
 
 

time: 16.5 us -> 15.1 us (0.915)
  local copies, waits for them, and re-layouts: 1.54 us -> 0.64 us
  Pallas kernels: 14.8 us -> 14.3 us
    unnamed x1, local copies, waits for them, and re-layouts: 1.54 us -> 0.64 us
    pallas_call x1, Pallas kernels: 14.8 us -> 14.3 us  [body(): pl.pallas_call(functools.partial(kernel, nx, ny, cx, cy, slots), out_shap...]
where the time goes in v3:
time: 15.1 us; the launch traced here: 14.9 us
  Pallas kernels  14.3 us (95%)
  local copies, waits for them, and re-layouts  0.64 us (4%)
    pallas_call x1, Pallas kernels, body(): pl.pallas_call(functools.partial(kernel, nx, ny, cx, cy, slots), out_shap...  14.3 us
    unnamed x1, local copies, waits for them, and re-layouts  0.64 us

profile of v3, /device:TPU:0, one launch (start us, length us, event | category | flops | bytes accessed | tf_op | source)
XLA Modules:
  0.0 14.9 jit_solution(300790212382961370)
XLA Ops:
  0.0 14.3 %shard_map.37 = f32[64,384]{1,0:T(8,128)S(1)} custom-call(f32[64,384]{1,0:T(8,128)} %field.1, f32[8,64]{1,0:T(8,128)} %bitcast.2, f32[8,48]{1,0:T(8,128)} %bitcast.3), custom_call_target="tpu_custom_call" | custom-call | tf_op jit(solution)/shard_map/pallas_call | solution.py:402
  14.3 0.6 %copy.5 = f32[64,384]{1,0:T(8,128)} copy(f32[64,384]{1,0:T(8,128)S(1)} %shard_map.37) | data formatting | bytes 196608
